TPU v7x, 512 devices: a whole 4x8x8 slice. The times are simulated.
512 devices in a mesh: blk: 64 (over y_lo, z, core), par: 8 (over x, y_hi).
Axes of the slice: x: 4, y: 8 (y_hi: 2, y_lo: 4; y = y_hi * 4 + y_lo), z: 8, core: 2. Of those that a mesh axis runs over, the one named last changes fastest.
Arguments:
- logder: float32 [8192, 6144], P('blk', 'par'), may hold values from -50 to 50
Outputs:
- kernel_tiles: float32 [64, 33, 128, 128], P('blk', None, 'par')
All inputs are finite; a program needn't handle non-finite values.
Results may differ from a plain program's by a relative error of at most 0.00015.
Values sent between devices are 32-bit elements; how exact they have to be, the bound alone decides.
A program may use at most 64 MiB of HBM per device.

v0:
```python
import math

import jax
import jax.numpy as jnp
from jax import lax
from jax.sharding import Mesh
from jax.sharding import PartitionSpec as P

PAR = ("par_0", "par_1")


def copy_for_each(value, axis):
    copies = jnp.broadcast_to(value, (lax.axis_size(axis), *value.shape))
    return lax.all_to_all(copies, axis, split_axis=0, concat_axis=0, tiled=True)


def over_copies(value, axis):
    return copy_for_each(value, axis).sum(axis=0)


def from_behind(value, axis, steps):
    count = lax.axis_size(axis)
    pairs = [(source, (source + steps) % count) for source in range(count)]
    return lax.ppermute(value, axis, pairs)


def summed_rows(value, axes, dim):
    if not axes:
        return value
    nearer = lax.psum_scatter(value, axes[0], scatter_dimension=dim, tiled=True)
    return summed_rows(nearer, axes[1:], dim)


def on_device(logder):
    nblocks = lax.axis_size("blk")
    nshards = lax.axis_size(PAR)
    rows, width = logder.shape
    totals = over_copies(jnp.sum(logder, axis=0), "blk")
    centered = logder - totals[None, :] / (rows * nblocks)
    factor = 1.0 / (width * nshards)
    half = nblocks // 2
    spacing = max(1, math.isqrt(half))
    plan = []
    for distance in range(half + 1):
        upper = spacing * -(-distance // spacing)
        plan.append((upper - distance, upper))
    needed = sorted(set([pair[0] for pair in plan] + [pair[1] for pair in plan]))
    blocks = {}
    for offset in needed:
        if offset == 0:
            blocks[offset] = centered
        else:
            blocks[offset] = from_behind(centered, "blk", -offset)
    lowers = sorted(set([pair[0] for pair in plan]))
    groups = []
    order = []
    for lower in lowers:
        picks = [distance for distance in range(half + 1) if plan[distance][0] == lower]
        others = jnp.stack([blocks[plan[distance][1]] for distance in picks])
        tiles = (
            jnp.einsum(
                "rp,kcp->krc",
                blocks[lower],
                others,
                precision=lax.Precision.HIGHEST,
                preferred_element_type=jnp.float32,
            )
            * factor
        )
        groups.append(tiles)
        order.append((lower, picks))
    shares = summed_rows(jnp.concatenate(groups, axis=0), PAR, 1)
    result = [None] * (half + 1)
    position = 0
    for lower, picks in order:
        group = shares[position : position + len(picks)]
        position = position + len(picks)
        if lower != 0:
            group = from_behind(group, "blk", lower)
        for place, distance in enumerate(picks):
            result[distance] = group[place]
    return jnp.stack(result)[None]


def solution(mesh):
    torus = Mesh(mesh.devices.reshape(mesh.shape["blk"], 4, 2), ("blk", "par_0", "par_1"))
    in_specs = (P("blk", PAR),)
    out_specs = P("blk", None, PAR, None)
    return jax.shard_map(
        on_device, mesh=torus, in_specs=in_specs, out_specs=out_specs, check_vma=False
    )
```

profile of v0, /device:TPU:1, one launch (start us, length us, event | category | flops | bytes accessed | tf_op | source)
XLA Modules:
  0.0 302.0 jit_solution(17991797873865255079)
XLA Ops:
  7.7 25.8 %all_to_all.6 = f32[64,1,768]{2,1,0:T(1,128)S(1)} all-to-all(f32[64,1,768]{2,1,0:T(1,128)S(1)} %broadcast_in_dim.7), channel_id=1, replica_groups=mesh['blk'=64,'par_0'=4,'par_1'=2] {'blk'}, dimensions={0} | all-to-all | bytes 393216 | tf_op jit(solution)/shard_map/all_to_all | solution.py:14
  34.6 5.3 %collective-permute-start = (f32[128,768]{1,0:T(8,128)S(1)}, f32[128,768]{1,0:T(8,128)S(1)}, u32[]{:S(2)}, u32[]{:S(2)}) collective-permute-start(f32[128,768]{1,0:T(8,128)S(1)} %get-tuple-element.6), channel_id=1, source_target_pairs={{0,472},{8,480},{16,488},{24,496},{32,504},{40,0},{48,8},{56,16},{... | collective-permute-start | bytes 1179656 | tf_op jit(solution)/shard_map/ppermute | solution.py:24
  39.9 4.0 %collective-permute-start.1 = (f32[128,768]{1,0:T(8,128)S(1)}, f32[128,768]{1,0:T(8,128)S(1)}, u32[]{:S(2)}, u32[]{:S(2)}) collective-permute-start(f32[128,768]{1,0:T(8,128)S(1)} %get-tuple-element.6), channel_id=1, source_target_pairs={{0,432},{8,440},{16,448},{24,456},{32,464},{40,472},{48,480},{56,4... | collective-permute-start | bytes 1179656 | tf_op jit(solution)/shard_map/ppermute | solution.py:24
  43.9 4.5 %collective-permute-start.2 = (f32[128,768]{1,0:T(8,128)S(1)}, f32[128,768]{1,0:T(8,128)S(1)}, u32[]{:S(2)}, u32[]{:S(2)}) collective-permute-start(f32[128,768]{1,0:T(8,128)S(1)} %get-tuple-element.6), channel_id=1, source_target_pairs={{0,392},{8,400},{16,408},{24,416},{32,424},{40,432},{48,440},{56,4... | collective-permute-start | bytes 1179656 | tf_op jit(solution)/shard_map/ppermute | solution.py:24
  48.4 3.0 collective-permute-start.3
  51.4 5.6 %collective-permute-start.4 = (f32[128,768]{1,0:T(8,128)S(1)}, f32[128,768]{1,0:T(8,128)S(1)}, u32[]{:S(2)}, u32[]{:S(2)}) collective-permute-start(f32[128,768]{1,0:T(8,128)S(1)} %get-tuple-element.6), channel_id=1, source_target_pairs={{0,312},{8,320},{16,328},{24,336},{32,344},{40,352},{48,360},{56,3... | collective-permute-start | bytes 1179656 | tf_op jit(solution)/shard_map/ppermute | solution.py:24
  57.0 8.0 %collective-permute-done = f32[128,768]{1,0:T(8,128)S(1)} collective-permute-done((f32[128,768]{1,0:T(8,128)S(1)}, f32[128,768]{1,0:T(8,128)S(1)}, u32[]{:S(2)}, u32[]{:S(2)}) %collective-permute-start) | collective-permute-done | bytes 393248 | tf_op jit(solution)/shard_map/ppermute | solution.py:24
  65.0 1.9 collective-permute-start.5
  67.1 24.2 %collective-permute-done.1 = f32[128,768]{1,0:T(8,128)S(1)} collective-permute-done((f32[128,768]{1,0:T(8,128)S(1)}, f32[128,768]{1,0:T(8,128)S(1)}, u32[]{:S(2)}, u32[]{:S(2)}) %collective-permute-start.1) | collective-permute-done | bytes 393248 | tf_op jit(solution)/shard_map/ppermute | solution.py:24
  91.3 2.7 collective-permute-start.6
  94.1 1.9 collective-permute-start.7
  96.1 11.0 %collective-permute-done.3 = f32[128,768]{1,0:T(8,128)S(1)} collective-permute-done((f32[128,768]{1,0:T(8,128)S(1)}, f32[128,768]{1,0:T(8,128)S(1)}, u32[]{:S(2)}, u32[]{:S(2)}) %collective-permute-start.3) | collective-permute-done | bytes 393248 | tf_op jit(solution)/shard_map/ppermute | solution.py:24
  107.1 7.7 %collective-permute-start.8 = (f32[128,768]{1,0:T(8,128)S(1)}, f32[128,768]{1,0:T(8,128)S(1)}, u32[]{:S(2)}, u32[]{:S(2)}) collective-permute-start(f32[128,768]{1,0:T(8,128)S(1)} %get-tuple-element.6), channel_id=1, source_target_pairs={{0,232},{8,240},{16,248},{24,256},{32,264},{40,272},{48,280},{56,2... | collective-permute-start | bytes 1179656 | tf_op jit(solution)/shard_map/ppermute | solution.py:24
  114.9 9.7 %collective-permute-done.4 = f32[128,768]{1,0:T(8,128)S(1)} collective-permute-done((f32[128,768]{1,0:T(8,128)S(1)}, f32[128,768]{1,0:T(8,128)S(1)}, u32[]{:S(2)}, u32[]{:S(2)}) %collective-permute-start.4) | collective-permute-done | bytes 393248 | tf_op jit(solution)/shard_map/ppermute | solution.py:24
  124.6 3.6 %collective-permute-start.9 = (f32[128,768]{1,0:T(8,128)S(1)}, f32[128,768]{1,0:T(8,128)S(1)}, u32[]{:S(2)}, u32[]{:S(2)}) collective-permute-start(f32[128,768]{1,0:T(8,128)S(1)} %get-tuple-element.6), channel_id=1, source_target_pairs={{0,488},{8,496},{16,504},{24,0},{32,8},{40,16},{48,24},{56,32},{64... | collective-permute-start | bytes 1179656 | tf_op jit(solution)/shard_map/ppermute | solution.py:24
  128.3 7.5 %collective-permute-done.5 = f32[128,768]{1,0:T(8,128)S(1)} collective-permute-done((f32[128,768]{1,0:T(8,128)S(1)}, f32[128,768]{1,0:T(8,128)S(1)}, u32[]{:S(2)}, u32[]{:S(2)}) %collective-permute-start.5) | collective-permute-done | bytes 393248 | tf_op jit(solution)/shard_map/ppermute | solution.py:24
  135.8 17.3 %collective-permute-start.10 = (f32[128,768]{1,0:T(8,128)S(1)}, f32[128,768]{1,0:T(8,128)S(1)}, u32[]{:S(2)}, u32[]{:S(2)}) collective-permute-start(f32[128,768]{1,0:T(8,128)S(1)} %get-tuple-element.6), channel_id=1, source_target_pairs={{0,480},{8,488},{16,496},{24,504},{32,0},{40,8},{48,16},{56,24},{6... | collective-permute-start | bytes 1179656 | tf_op jit(solution)/shard_map/ppermute | solution.py:24
  153.2 2.3 fusion.5
  155.5 2.0 fusion.9
  157.5 2.0 fusion.7
  159.5 5.7 %collective-permute-done.9 = f32[128,768]{1,0:T(8,128)S(1)} collective-permute-done((f32[128,768]{1,0:T(8,128)S(1)}, f32[128,768]{1,0:T(8,128)S(1)}, u32[]{:S(2)}, u32[]{:S(2)}) %collective-permute-start.9) | collective-permute-done | bytes 393248 | tf_op jit(solution)/shard_map/ppermute | solution.py:24
  165.3 2.3 fusion.3
  167.6 7.4 %collective-permute-done.10 = f32[128,768]{1,0:T(8,128)S(1)} collective-permute-done((f32[128,768]{1,0:T(8,128)S(1)}, f32[128,768]{1,0:T(8,128)S(1)}, u32[]{:S(2)}, u32[]{:S(2)}) %collective-permute-start.10) | collective-permute-done | bytes 393248 | tf_op jit(solution)/shard_map/ppermute | solution.py:24
  175.0 2.3 fusion.1
  177.3 2.3 copy.72
  179.6 59.5 %reduce-scatter.3.cloned.1.call-done = f32[33,32,128]{2,0,1:T(8,128)} async-done(((f32[33,128,128]{2,0,1:T(8,128)}), f32[33,32,128]{2,0,1:T(8,128)}) %reduce-scatter.3.cloned.1.call-update) | async-done | bytes 540688 | tf_op jit(solution)/shard_map/reduce_scatter | solution.py:30
  239.1 34.4 %reduce-scatter.5.cloned.1.call-done = f32[33,16,128]{2,0,1:T(8,128)} async-done(((f32[33,32,128]{2,0,1:T(8,128)}), f32[33,16,128]{2,0,1:T(8,128)}) %reduce-scatter.5.cloned.1.call-update) | async-done | bytes 270352 | tf_op jit(solution)/shard_map/reduce_scatter | solution.py:30
  274.5 3.3 %collective-permute-start.13 = (f32[6,16,128]{2,0,1:T(8,128)S(1)}, f32[6,16,128]{2,0,1:T(8,128)S(1)}, u32[]{:S(2)}, u32[]{:S(2)}) collective-permute-start(f32[6,16,128]{2,0,1:T(8,128)S(1)} %get-tuple-element.33), channel_id=1, source_target_pairs={{0,16},{8,24},{16,32},{24,40},{32,48},{40,56},{48,64},{56,72},{64,... | collective-permute-start | bytes 147464 | tf_op jit(solution)/shard_map/ppermute | solution.py:24
  277.8 1.4 fusion.15
  280.2 4.4 %collective-permute-start.11 = (f32[7,16,128]{2,0,1:T(8,128)S(1)}, f32[7,16,128]{2,0,1:T(8,128)S(1)}, u32[]{:S(2)}, u32[]{:S(2)}) collective-permute-start(f32[7,16,128]{2,0,1:T(8,128)S(1)} %get-tuple-element.35), channel_id=1, source_target_pairs={{0,32},{8,40},{16,48},{24,56},{32,64},{40,72},{48,80},{56,88},{64,... | collective-permute-start | bytes 172040 | tf_op jit(solution)/shard_map/ppermute | solution.py:24
  284.6 6.0 %collective-permute-start.12 = (f32[7,16,128]{2,0,1:T(8,128)S(1)}, f32[7,16,128]{2,0,1:T(8,128)S(1)}, u32[]{:S(2)}, u32[]{:S(2)}) collective-permute-start(f32[7,16,128]{2,0,1:T(8,128)S(1)} %get-tuple-element.34), channel_id=1, source_target_pairs={{0,24},{8,32},{16,40},{24,48},{32,56},{40,64},{48,72},{56,80},{64,... | collective-permute-start | bytes 172040 | tf_op jit(solution)/shard_map/ppermute | solution.py:24
  290.6 1.9 collective-permute-start.14
  (65 shorter events, 7.3 us)
Async XLA Ops:
  6.5 232.6 %reduce-scatter.3.cloned.1.call-start = ((), (), s32[]{:S(2)}) async-start(), calls=%async_computation.3 | async-start | bytes 3276800 | tf_op jit(solution)/shard_map/reduce_scatter | solution.py:30
  34.6 30.4 %collective-permute-start = (f32[128,768]{1,0:T(8,128)S(1)}, f32[128,768]{1,0:T(8,128)S(1)}, u32[]{:S(2)}, u32[]{:S(2)}) collective-permute-start(f32[128,768]{1,0:T(8,128)S(1)} %get-tuple-element.6), channel_id=1, source_target_pairs={{0,472},{8,480},{16,488},{24,496},{32,504},{40,0},{48,8},{56,16},{... | collective-permute-start | bytes 1179656 | tf_op jit(solution)/shard_map/ppermute | solution.py:24
  39.9 51.4 %collective-permute-start.1 = (f32[128,768]{1,0:T(8,128)S(1)}, f32[128,768]{1,0:T(8,128)S(1)}, u32[]{:S(2)}, u32[]{:S(2)}) collective-permute-start(f32[128,768]{1,0:T(8,128)S(1)} %get-tuple-element.6), channel_id=1, source_target_pairs={{0,432},{8,440},{16,448},{24,456},{32,464},{40,472},{48,480},{56,4... | collective-permute-start | bytes 1179656 | tf_op jit(solution)/shard_map/ppermute | solution.py:24
  43.9 50.1 %collective-permute-start.2 = (f32[128,768]{1,0:T(8,128)S(1)}, f32[128,768]{1,0:T(8,128)S(1)}, u32[]{:S(2)}, u32[]{:S(2)}) collective-permute-start(f32[128,768]{1,0:T(8,128)S(1)} %get-tuple-element.6), channel_id=1, source_target_pairs={{0,392},{8,400},{16,408},{24,416},{32,424},{40,432},{48,440},{56,4... | collective-permute-start | bytes 1179656 | tf_op jit(solution)/shard_map/ppermute | solution.py:24
  48.4 58.7 %collective-permute-start.3 = (f32[128,768]{1,0:T(8,128)S(1)}, f32[128,768]{1,0:T(8,128)S(1)}, u32[]{:S(2)}, u32[]{:S(2)}) collective-permute-start(f32[128,768]{1,0:T(8,128)S(1)} %get-tuple-element.6), channel_id=1, source_target_pairs={{0,352},{8,360},{16,368},{24,376},{32,384},{40,392},{48,400},{56,4... | collective-permute-start | bytes 1179656 | tf_op jit(solution)/shard_map/ppermute | solution.py:24
  51.4 73.2 %collective-permute-start.4 = (f32[128,768]{1,0:T(8,128)S(1)}, f32[128,768]{1,0:T(8,128)S(1)}, u32[]{:S(2)}, u32[]{:S(2)}) collective-permute-start(f32[128,768]{1,0:T(8,128)S(1)} %get-tuple-element.6), channel_id=1, source_target_pairs={{0,312},{8,320},{16,328},{24,336},{32,344},{40,352},{48,360},{56,3... | collective-permute-start | bytes 1179656 | tf_op jit(solution)/shard_map/ppermute | solution.py:24
  65.0 70.7 %collective-permute-start.5 = (f32[128,768]{1,0:T(8,128)S(1)}, f32[128,768]{1,0:T(8,128)S(1)}, u32[]{:S(2)}, u32[]{:S(2)}) collective-permute-start(f32[128,768]{1,0:T(8,128)S(1)} %get-tuple-element.6), channel_id=1, source_target_pairs={{0,272},{8,280},{16,288},{24,296},{32,304},{40,312},{48,320},{56,3... | collective-permute-start | bytes 1179656 | tf_op jit(solution)/shard_map/ppermute | solution.py:24
  91.3 64.2 %collective-permute-start.6 = (f32[128,768]{1,0:T(8,128)S(1)}, f32[128,768]{1,0:T(8,128)S(1)}, u32[]{:S(2)}, u32[]{:S(2)}) collective-permute-start(f32[128,768]{1,0:T(8,128)S(1)} %get-tuple-element.6), channel_id=1, source_target_pairs={{0,504},{8,0},{16,8},{24,16},{32,24},{40,32},{48,40},{56,48},{64,5... | collective-permute-start | bytes 1179656 | tf_op jit(solution)/shard_map/ppermute | solution.py:24
  94.1 63.4 %collective-permute-start.7 = (f32[128,768]{1,0:T(8,128)S(1)}, f32[128,768]{1,0:T(8,128)S(1)}, u32[]{:S(2)}, u32[]{:S(2)}) collective-permute-start(f32[128,768]{1,0:T(8,128)S(1)} %get-tuple-element.6), channel_id=1, source_target_pairs={{0,496},{8,504},{16,0},{24,8},{32,16},{40,24},{48,32},{56,40},{64,... | collective-permute-start | bytes 1179656 | tf_op jit(solution)/shard_map/ppermute | solution.py:24
  107.1 52.4 %collective-permute-start.8 = (f32[128,768]{1,0:T(8,128)S(1)}, f32[128,768]{1,0:T(8,128)S(1)}, u32[]{:S(2)}, u32[]{:S(2)}) collective-permute-start(f32[128,768]{1,0:T(8,128)S(1)} %get-tuple-element.6), channel_id=1, source_target_pairs={{0,232},{8,240},{16,248},{24,256},{32,264},{40,272},{48,280},{56,2... | collective-permute-start | bytes 1179656 | tf_op jit(solution)/shard_map/ppermute | solution.py:24
  124.6 40.6 %collective-permute-start.9 = (f32[128,768]{1,0:T(8,128)S(1)}, f32[128,768]{1,0:T(8,128)S(1)}, u32[]{:S(2)}, u32[]{:S(2)}) collective-permute-start(f32[128,768]{1,0:T(8,128)S(1)} %get-tuple-element.6), channel_id=1, source_target_pairs={{0,488},{8,496},{16,504},{24,0},{32,8},{40,16},{48,24},{56,32},{64... | collective-permute-start | bytes 1179656 | tf_op jit(solution)/shard_map/ppermute | solution.py:24
  135.8 39.2 %collective-permute-start.10 = (f32[128,768]{1,0:T(8,128)S(1)}, f32[128,768]{1,0:T(8,128)S(1)}, u32[]{:S(2)}, u32[]{:S(2)}) collective-permute-start(f32[128,768]{1,0:T(8,128)S(1)} %get-tuple-element.6), channel_id=1, source_target_pairs={{0,480},{8,488},{16,496},{24,504},{32,0},{40,8},{48,16},{56,24},{6... | collective-permute-start | bytes 1179656 | tf_op jit(solution)/shard_map/ppermute | solution.py:24
  179.6 93.9 %reduce-scatter.5.cloned.1.call-start = ((), (), s32[]{:S(2)}) async-start(), calls=%async_computation.4 | async-start | bytes 983040 | tf_op jit(solution)/shard_map/reduce_scatter | solution.py:30
  274.5 18.0 %collective-permute-start.13 = (f32[6,16,128]{2,0,1:T(8,128)S(1)}, f32[6,16,128]{2,0,1:T(8,128)S(1)}, u32[]{:S(2)}, u32[]{:S(2)}) collective-permute-start(f32[6,16,128]{2,0,1:T(8,128)S(1)} %get-tuple-element.33), channel_id=1, source_target_pairs={{0,16},{8,24},{16,32},{24,40},{32,48},{40,56},{48,64},{56,72},{64,... | collective-permute-start | bytes 147464 | tf_op jit(solution)/shard_map/ppermute | solution.py:24
  280.2 13.7 %collective-permute-start.11 = (f32[7,16,128]{2,0,1:T(8,128)S(1)}, f32[7,16,128]{2,0,1:T(8,128)S(1)}, u32[]{:S(2)}, u32[]{:S(2)}) collective-permute-start(f32[7,16,128]{2,0,1:T(8,128)S(1)} %get-tuple-element.35), channel_id=1, source_target_pairs={{0,32},{8,40},{16,48},{24,56},{32,64},{40,72},{48,80},{56,88},{64,... | collective-permute-start | bytes 172040 | tf_op jit(solution)/shard_map/ppermute | solution.py:24
  284.6 9.5 %collective-permute-start.12 = (f32[7,16,128]{2,0,1:T(8,128)S(1)}, f32[7,16,128]{2,0,1:T(8,128)S(1)}, u32[]{:S(2)}, u32[]{:S(2)}) collective-permute-start(f32[7,16,128]{2,0,1:T(8,128)S(1)} %get-tuple-element.34), channel_id=1, source_target_pairs={{0,24},{8,32},{16,40},{24,48},{32,56},{40,64},{48,72},{56,80},{64,... | collective-permute-start | bytes 172040 | tf_op jit(solution)/shard_map/ppermute | solution.py:24
  290.6 3.2 %collective-permute-start.14 = (f32[6,16,128]{2,0,1:T(8,128)S(1)}, f32[6,16,128]{2,0,1:T(8,128)S(1)}, u32[]{:S(2)}, u32[]{:S(2)}) collective-permute-start(f32[6,16,128]{2,0,1:T(8,128)S(1)} %get-tuple-element.32), channel_id=1, source_target_pairs={{0,8},{8,16},{16,24},{24,32},{32,40},{40,48},{48,56},{56,64},{64,7... | collective-permute-start | bytes 147464 | tf_op jit(solution)/shard_map/ppermute | solution.py:24
  294.5 0.7 copy-start
Sparse Core Ops, SparseCore 0:
  179.7 59.3 reduce-scatter.2
  241.9 31.5 reduce-scatter.4
where the time goes:
time: 307 us; the launch traced here: 302 us
  waiting for transfers between devices  169 us (55%)
  starting transfers between devices  73 us (24%)
  blocking collectives  25.8 us (8%)
  between operations  14 us (5%)
  matrix products  10.9 us (4%)
  local copies, waits for them, and re-layouts  7.25 us (2%)
    reduce_scatter x2, waiting for transfers between devices, summed_rows(): nearer = lax.psum_scatter(value, axes[0], scatter_dimension=dim, tiled=True)  93.9 us
    ppermute x15, waiting for transfers between devices, from_behind(): return lax.ppermute(value, axis, pairs)  75 us
    ppermute x15, starting transfers between devices, from_behind(): return lax.ppermute(value, axis, pairs)  73 us
    all_to_all x1, blocking collectives, copy_for_each(): return lax.all_to_all(copies, axis, split_axis=0, concat_axis=0, tiled=True)  25.8 us
    dot_general x5, matrix products, on_device(): jnp.einsum('rp,kcp->krc', blocks[lower], others, precision=lax.Precision....  10.9 us
  transfers between devices with their start and end apart: 17, of which 11 were waited for; matrix products, arithmetic and copies ran while one was open for 4% of the time, Pallas kernels for 0%

commit v1 on v0

v1 whole, which is shorter than its diff:
```python
import jax
import jax.numpy as jnp
from jax import lax
from jax.experimental import pallas as pl
from jax.experimental.pallas import tpu as pltpu
from jax.sharding import Mesh
from jax.sharding import PartitionSpec as P

MESH = pl.DeviceIdType.MESH

ROWS, WIDTH = 128, 768
LANES = 128
COLS = WIDTH // LANES
NCH = 4
CH = ROWS // NCH
NB = 64
HALF = 32
NSAMPLES = 8192
NPARAMS = 6144

NSLOT = 12
UP = {1: 5, 2: 6, 3: 7, 4: 8}
DOWN = {1: 9, 2: 10, 3: 11}

GROUPS = [(0, 6), (6, 8), (14, 8), (22, 8), (30, 5)]
NTILE = 35


def rem(value, count):
    return lax.rem(value, jnp.int32(count))


def div(value, count):
    return lax.div(value, jnp.int32(count))


def kernel(
    x_ref, out_ref, raw, hi, lo, zs, zt, ys, mean, pk, pr, sx, xr, fb,
    own_send, y_send, y_recv, z_send, z_own, z_recv, ms_send, ms_recv, mt_send, mt_recv,
    d_send, d_recv, x_send, x_recv, f_send, f_recv,
):
    a = lax.axis_index("a")
    z = lax.axis_index("z")
    c = lax.axis_index("c")
    x = lax.axis_index("x")
    h = lax.axis_index("h")
    y = h * 4 + a
    first = c == h
    other = c != h

    def at_y(steps, core):
        yy = rem(y + 8 + steps, 8)
        return (rem(yy, 4), z, core, x, div(yy, 4))

    def at_z(steps):
        return (a, rem(z + 8 + steps, 8), c, x, h)

    def at_x(steps):
        return (a, z, c, rem(x + steps, 4), h)

    partner = (a, z, 1 - c, x, h)

    def remote(src, dst, send, recv, device):
        return pltpu.make_async_remote_copy(
            src_ref=src, dst_ref=dst, send_sem=send, recv_sem=recv,
            device_id=device, device_id_type=MESH,
        )

    def landed(ref, sem):
        pltpu.make_async_copy(ref, ref, sem).wait()

    barrier = pltpu.get_barrier_semaphore()

    def hello(device):
        pl.semaphore_signal(barrier, inc=1, device_id=device, device_id_type=MESH)

    hello(partner)
    for k in range(1, 8):
        hello(at_z(k))
        hello(at_y(k, 0))
        hello(at_y(k, 1))
    for k in range(1, 4):
        hello(at_x(k))
    pl.semaphore_wait(barrier, 25)

    def part(i):
        return pl.ds(pl.multiple_of(i * CH, CH), CH)

    def from_below(r):
        return div(rem(y + 8 - r, 8), 4) == c

    def y_own_up(i):
        return remote(x_ref.at[part(i)], raw.at[1, part(i)], own_send.at[0, i], y_recv.at[1, i], at_y(1, c))

    def y_own_down(i):
        return remote(
            x_ref.at[part(i)], raw.at[3, part(i)], own_send.at[0, i], y_recv.at[3, i], at_y(-1, 1 - c)
        )

    def y_own_partner(i):
        return remote(x_ref.at[part(i)], raw.at[4, part(i)], own_send.at[1, i], y_recv.at[4, i], partner)

    def y_relay(r, up, i):
        to = r + 1 if up else r - 1
        return remote(
            raw.at[r, part(i)], raw.at[to, part(i)], y_send.at[r, i], y_recv.at[to, i],
            at_y(1 if up else -1, c),
        )

    def z_start(src, i, low):
        to = UP[1] if low else DOWN[1]
        return remote(
            src.at[part(i)], raw.at[to, part(i)], z_own.at[0 if low else 1, i], z_recv.at[to - 5, i],
            at_z(-1 if low else 1),
        )

    def z_relay(slot, to, i, low):
        return remote(
            raw.at[slot, part(i)], raw.at[to, part(i)], z_send.at[slot - 5, i], z_recv.at[to - 5, i],
            at_z(-1 if low else 1),
        )

    def y_event(dist, i):
        @pl.when(from_below(dist))
        def _():
            landed(raw.at[dist, part(i)], y_recv.at[dist, i])
            if dist < 4:
                y_relay(dist, True, i).start()

        slot = 4 - dist

        @pl.when(jnp.logical_not(from_below(slot)))
        def _():
            landed(raw.at[slot, part(i)], y_recv.at[slot, i])
            if dist < 4:
                y_relay(slot, False, i).start()

    def z_event(k, i):
        if k < 4:
            landed(raw.at[UP[k], part(i)], z_recv.at[UP[k] - 5, i])
            if k < 3:
                z_relay(UP[k], UP[k + 1], i, True).start()
            else:
                @pl.when(i < NCH // 2)
                def _():
                    z_relay(UP[3], UP[4], i, True).start()
            landed(raw.at[DOWN[k], part(i)], z_recv.at[DOWN[k] - 5, i])
            if k < 3:
                z_relay(DOWN[k], DOWN[k + 1], i, False).start()
            else:
                @pl.when(i >= NCH // 2)
                def _():
                    z_relay(DOWN[3], UP[4], i, False).start()
        else:
            landed(raw.at[UP[4], part(i)], z_recv.at[UP[4] - 5, i])

    def each(body):
        lax.fori_loop(0, NCH, lambda i, _: (body(i), 0)[1], 0)

    @pl.when(first)
    def _():
        def go(i):
            y_own_up(i).start()
            z_start(x_ref, i, True).start()
            z_start(x_ref, i, False).start()
        each(go)

    @pl.when(other)
    def _():
        def go(i):
            y_own_down(i).start()
            y_own_partner(i).start()
        each(go)

    sums = jnp.sum(x_ref[...], axis=0, keepdims=True)
    zs[z] = jnp.zeros((8, LANES), jnp.float32)
    for k in range(COLS):
        zs[z, k : k + 1, :] = sums[:, k * LANES : (k + 1) * LANES]

    def ms_copy(k):
        return remote(zs.at[z], zs.at[z], ms_send.at[k - 1], ms_recv.at[k - 1], at_z(k))

    for k in range(1, 8):
        ms_copy(k).start()

    def phase_one(dist):
        def step(i):
            y_event(dist, i)

            @pl.when(first)
            def _():
                z_event(dist, i)

            if dist == 4:
                @pl.when(other)
                def _():
                    z_start(raw.at[0], i, True).start()
                    z_start(raw.at[0], i, False).start()
        each(step)

    phase_one(1)

    mine = 2 * a + c

    def mt_copy(k):
        return remote(zt, ys.at[mine], mt_send.at[k], mt_recv.at[mine], at_y(k, h))

    for k in range(1, 8):
        source = rem(z + 8 - k, 8)
        landed(zs.at[source], ms_recv.at[k - 1])
    total = zs[0]
    for k in range(1, 8):
        total = total + zs[k]
    zt[...] = total
    for k in range(1, 8):
        mt_copy(k).start()

    @pl.when(first)
    def _():
        ys[mine] = total

    @pl.when(other)
    def _():
        mt_copy(0).start()

    for dist in range(2, 5):
        phase_one(dist)

    @pl.when(first)
    def _():
        each(lambda i: landed(raw.at[4, part(i)], y_recv.at[4, i]))
        raw[0] = x_ref[...]

    for k in range(8):
        @pl.when(jnp.logical_or(other, mine != k))
        def _():
            landed(ys.at[k], mt_recv.at[k])
    total = ys[0]
    for k in range(1, 8):
        total = total + ys[k]
    mean[...] = total * (1.0 / NSAMPLES)

    def convert(slot):
        m = mean[...]
        row = jnp.concatenate([m[k : k + 1, :] for k in range(COLS)], axis=1)
        value = raw[slot] - row
        top = value.astype(jnp.bfloat16)
        hi[slot] = top
        lo[slot] = (value - top.astype(jnp.float32)).astype(jnp.bfloat16)

    lax.fori_loop(0, 5, lambda s, _: (convert(s), 0)[1], 0)

    e_mine = y

    def pair(r, j):
        e_low = rem(e_mine + 8 - r, 8)
        low = 16 * rem(e_low, 4) + 2 * z + div(e_low, 4)
        z_high = rem(z + 8 + j, 8)
        high = 16 * a + 2 * z_high + h
        gap = rem(high + NB - low, NB)
        keep = gap <= HALF
        a_row = jnp.where(keep, rem(e_low, 4), a)
        z_row = jnp.where(keep, z, z_high)
        c_row = jnp.where(keep, div(e_low, 4), h)
        d = jnp.where(keep, gap, NB - gap)
        return keep, gap, (a_row, z_row, c_row), d

    def slot_of(j):
        return jnp.where(j >= 0, jnp.where(j == 0, 0, 4 + j), 8 - j)

    def tile_of(k, t):
        if k == 0:
            return jnp.where(t == 5, 2, t), jnp.int32(0) * t, t == 5
        if k == 4:
            return t, 4 + jnp.int32(0) * t, t < 0
        return jnp.where(t < 5, t, t - 4), jnp.where(t < 5, k, -k), t < 0

    contract = (((1,), (1,)), ((), ()))

    def dot(p, q):
        return lax.dot_general(p, q, contract, preferred_element_type=jnp.float32)

    def compute(k, t):
        r, j, swap = tile_of(k, t)
        keep, _, _, _ = pair(r, j)
        keep = jnp.logical_xor(keep, swap)
        row = jnp.where(keep, r, slot_of(j))
        col = jnp.where(keep, slot_of(j), r)
        acc = dot(hi[row], hi[col]) + dot(hi[row], lo[col]) + dot(lo[row], hi[col])
        index = GROUPS[k][0] + t
        for xx in range(4):
            for yy in range(2):
                start = 32 * xx + 16 * yy
                pk[yy, xx, index] = acc[start : start + 16, :]

    def d_copy(k):
        t0, n = GROUPS[k]
        return remote(
            pk.at[1 - c, :, pl.ds(t0, n)], pr.at[:, pl.ds(t0, n)], d_send.at[k], d_recv.at[k], partner
        )

    def x_copy(k, s):
        t0, n = GROUPS[k]
        return remote(
            sx.at[rem(x + s, 4), pl.ds(t0, n)], xr.at[s - 1, pl.ds(t0, n)],
            x_send.at[k, s - 1], x_recv.at[k, s - 1], at_x(s),
        )

    def over_cores(k):
        t0, n = GROUPS[k]
        landed(pr.at[:, pl.ds(t0, n)], d_recv.at[k])
        sx[:, t0 : t0 + n] = pk[c, :, t0 : t0 + n] + pr[:, t0 : t0 + n]
        for s in range(1, 4):
            x_copy(k, s).start()

    def target(k, t):
        r, j, swap = tile_of(k, t)
        keep, gap, (a_row, z_row, c_row), d = pair(r, j)
        valid = jnp.logical_not(jnp.logical_and(swap, gap != HALF))
        low = jnp.logical_and(r == 0, j == 4)
        valid = jnp.logical_and(valid, jnp.logical_or(jnp.logical_not(low), z < 4))
        low = jnp.logical_and(r == 4, j == 0)
        valid = jnp.logical_and(valid, jnp.logical_or(jnp.logical_not(low), h == 0))
        low = jnp.logical_and(r == 4, j == 4)
        valid = jnp.logical_and(valid, jnp.logical_or(jnp.logical_not(low), h == 1))
        a_row = jnp.where(swap, a, a_row)
        z_row = jnp.where(swap, z, z_row)
        c_row = jnp.where(swap, h, c_row)
        local = (a_row == a) & (z_row == z) & (c_row == c) & (c == h)
        return valid, local, (a_row, z_row, c_row, x, c), d

    def f_copy(k, t):
        _, _, device, d = target(k, t)
        index = GROUPS[k][0] + t
        return remote(fb.at[index], out_ref.at[0, d], f_send.at[index], f_recv.at[d], device)

    def over_planes(k):
        t0, n = GROUPS[k]
        for s in range(1, 4):
            landed(xr.at[s - 1, pl.ds(t0, n)], x_recv.at[k, s - 1])
        block = pl.ds(t0, n)
        fb[block] = (sx[x, block] + xr[0, block] + xr[1, block] + xr[2, block]) * (1.0 / NPARAMS)

        def send(t, carry):
            valid, local, _, d = target(k, t)

            @pl.when(jnp.logical_and(valid, local))
            def _():
                out_ref[0, d] = fb[t0 + t]

            @pl.when(jnp.logical_and(valid, jnp.logical_not(local)))
            def _():
                f_copy(k, t).start()

            return carry

        lax.fori_loop(0, n, send, 0)

    for k in range(5):
        if 1 <= k <= 3:
            convert(UP[k])
            convert(DOWN[k])
        if k == 4:
            convert(UP[4])
        n = GROUPS[k][1]
        per = -(-n // NCH)

        def step(i):
            if k < 4:
                @pl.when(other)
                def _():
                    z_event(k + 1, i)
            for u in range(per):
                if per * NCH <= n:
                    compute(k, i * per + u)
                else:
                    @pl.when(i * per + u < n)
                    def _():
                        compute(k, i * per + u)

        each(step)
        d_copy(k).start()
        over_cores(k)
        if k:
            over_planes(k - 1)
    over_planes(4)

    def arrived(d, carry):
        step = div(d, 2)
        local = (rem(d, 2) == 0) & (step <= 4) & (z + step <= 7)
        for r in range(1, 5):
            _, gap, _, _ = pair(r, 0)
            here = (gap >= HALF) & (d == NB - gap)
            local = local | ((here & (h == 0)) if r == 4 else here)
        local = local & first

        @pl.when(jnp.logical_not(local))
        def _():
            landed(out_ref.at[0, d], f_recv.at[d])

        return carry

    lax.fori_loop(0, HALF + 1, arrived, 0)

    def sent(i):
        @pl.when(first)
        def _():
            y_own_up(i).wait_send()

        @pl.when(other)
        def _():
            y_own_down(i).wait_send()
            y_own_partner(i).wait_send()

        z_start(x_ref, i, True).wait_send()
        z_start(x_ref, i, False).wait_send()
        for dist in range(1, 4):
            @pl.when(from_below(dist))
            def _():
                y_relay(dist, True, i).wait_send()

            @pl.when(jnp.logical_not(from_below(4 - dist)))
            def _():
                y_relay(4 - dist, False, i).wait_send()
        for k in range(1, 3):
            z_relay(UP[k], UP[k + 1], i, True).wait_send()
            z_relay(DOWN[k], DOWN[k + 1], i, False).wait_send()

        @pl.when(i < NCH // 2)
        def _():
            z_relay(UP[3], UP[4], i, True).wait_send()

        @pl.when(i >= NCH // 2)
        def _():
            z_relay(DOWN[3], UP[4], i, False).wait_send()

    each(sent)
    for k in range(1, 8):
        ms_copy(k).wait_send()
        mt_copy(k).wait_send()

    @pl.when(other)
    def _():
        mt_copy(0).wait_send()

    for k in range(5):
        d_copy(k).wait_send()
        for s in range(1, 4):
            x_copy(k, s).wait_send()

        def gone(t, carry):
            valid, local, _, _ = target(k, t)

            @pl.when(jnp.logical_and(valid, jnp.logical_not(local)))
            def _():
                f_copy(k, t).wait_send()

            return carry

        lax.fori_loop(0, GROUPS[k][1], gone, 0)


def on_device(logder):
    f32, bf16 = jnp.float32, jnp.bfloat16
    dma = pltpu.SemaphoreType.DMA
    return pl.pallas_call(
        kernel,
        out_shape=jax.ShapeDtypeStruct((1, HALF + 1, 16, ROWS), f32),
        in_specs=[pl.BlockSpec(memory_space=pltpu.VMEM)],
        out_specs=pl.BlockSpec(memory_space=pltpu.VMEM),
        scratch_shapes=[
            pltpu.VMEM((NSLOT, ROWS, WIDTH), f32),
            pltpu.VMEM((NSLOT, ROWS, WIDTH), bf16),
            pltpu.VMEM((NSLOT, ROWS, WIDTH), bf16),
            pltpu.VMEM((8, 8, LANES), f32),
            pltpu.VMEM((8, LANES), f32),
            pltpu.VMEM((8, 8, LANES), f32),
            pltpu.VMEM((8, LANES), f32),
            pltpu.VMEM((2, 4, NTILE, 16, ROWS), f32),
            pltpu.VMEM((4, NTILE, 16, ROWS), f32),
            pltpu.VMEM((4, NTILE, 16, ROWS), f32),
            pltpu.VMEM((3, NTILE, 16, ROWS), f32),
            pltpu.VMEM((NTILE, 16, ROWS), f32),
            dma((2, NCH)),
            dma((5, NCH)),
            dma((5, NCH)),
            dma((7, NCH)),
            dma((2, NCH)),
            dma((7, NCH)),
            dma((7,)),
            dma((7,)),
            dma((8,)),
            dma((8,)),
            dma((5,)),
            dma((5,)),
            dma((5, 3)),
            dma((5, 3)),
            dma((NTILE,)),
            dma((HALF + 1,)),
        ],
        compiler_params=pltpu.CompilerParams(collective_id=0, has_side_effects=True),
    )(logder)


def solution(mesh):
    torus = Mesh(mesh.devices.reshape(4, 8, 2, 4, 2), ("a", "z", "c", "x", "h"))
    return jax.shard_map(
        on_device,
        mesh=torus,
        in_specs=(P(("a", "z", "c"), ("x", "h")),),
        out_specs=P(("a", "z", "c"), None, ("x", "h"), None),
        check_vma=False,
    )
```

time: 307 us -> 80.1 us (0.26); the launches traced: 302 us -> 79.9 us
  waiting for transfers between devices: 169 us -> 0 us
  Pallas kernels: 0 us -> 78.2 us
  starting transfers between devices: 73 us -> 0 us
  blocking collectives: 25.8 us -> 0 us
  between operations: 14 us -> 0.01 us
  matrix products: 10.9 us -> 0 us
  local copies, waits for them, and re-layouts: 7.25 us -> 1.68 us
    reduce_scatter x2 -> x0, waiting for transfers between devices: 93.9 us -> none  [summed_rows(): nearer = lax.psum_scatter(value, axes[0], scatter_dimension=dim, tiled=True)]
    pallas_call x0 -> x1, Pallas kernels: none -> 78.2 us  [on_device(): pl.pallas_call(kernel, out_shape=jax.ShapeDtypeStruct((1, HALF + 1, 16, R...]
    ppermute x15 -> x0, waiting for transfers between devices: 75 us -> none  [from_behind(): return lax.ppermute(value, axis, pairs)]
    ppermute x15 -> x0, starting transfers between devices: 73 us -> none  [from_behind(): return lax.ppermute(value, axis, pairs)]
    all_to_all x1 -> x0, blocking collectives: 25.8 us -> none  [copy_for_each(): return lax.all_to_all(copies, axis, split_axis=0, concat_axis=0, tiled=True)]
    dot_general x5 -> x0, matrix products: 10.9 us -> none  [on_device(): jnp.einsum('rp,kcp->krc', blocks[lower], others, precision=lax.Precision....]
    slice x7 -> x0, local copies, waits for them, and re-layouts: 3.54 us -> none  [the longest x2 2 us: on_device(): group = shares[position:position + len(picks)]]
  transfers between devices with their start and end apart: 17 -> 0, of which waited for: 11 -> 0; matrix products, arithmetic and copies ran while one was open for 4% -> 0% of each run, Pallas kernels for 0% -> 0%
where the time goes in v1:
time: 80.1 us; the launch traced here: 79.9 us
  Pallas kernels  78.2 us (98%)
  local copies, waits for them, and re-layouts  1.68 us (2%)
    pallas_call x1, Pallas kernels, on_device(): pl.pallas_call(kernel, out_shape=jax.ShapeDtypeStruct((1, HALF + 1, 16, R...  78.2 us
    unnamed x1, local copies, waits for them, and re-layouts  1.68 us

profile of v1, /device:TPU:1, one launch (start us, length us, event | category | flops | bytes accessed | tf_op | source)
XLA Modules:
  0.0 79.9 jit_solution(89750880372494586)
XLA Ops:
  0.0 78.2 %shard_map.17 = f32[1,33,16,128]{3,2,1,0:T(8,128)} custom-call(f32[128,768]{1,0:T(8,128)} %x_ref.1), custom_call_target="tpu_custom_call" | custom-call | tf_op jit(solution)/shard_map/pallas_call | solution.py:466
  78.2 1.7 %copy.3 = f32[1,33,16,128]{3,2,1,0:T(8,128)} copy(f32[1,33,16,128]{3,2,1,0:T(8,128)} %shard_map.17) | data formatting | bytes 540672

commit v2 on v1

--- a/solution.py
+++ b/solution.py
@@ -16,6 +16,7 @@
 NB = 64
 HALF = 32
 NSAMPLES = 8192
+SUMS_AT = 2
 NPARAMS = 6144
 
 NSLOT = 12
@@ -35,9 +36,9 @@
 
 
 def kernel(
-    x_ref, out_ref, raw, hi, lo, zs, zt, ys, mean, pk, pr, sx, xr, fb,
+    x_ref, out_ref, raw, hi, lo, zs, zt, ys, mean, pk, pr, xr, fb, home,
     own_send, y_send, y_recv, z_send, z_own, z_recv, ms_send, ms_recv, mt_send, mt_recv,
-    d_send, d_recv, x_send, x_recv, f_send, f_recv,
+    known, d_send, d_recv, x_send, x_recv, f_send, f_recv, g_send, g_recv,
 ):
     a = lax.axis_index("a")
     z = lax.axis_index("z")
@@ -75,13 +76,21 @@
         pl.semaphore_signal(barrier, inc=1, device_id=device, device_id_type=MESH)
 
     hello(partner)
-    for k in range(1, 8):
+    for k in (1, 7):
         hello(at_z(k))
         hello(at_y(k, 0))
         hello(at_y(k, 1))
     for k in range(1, 4):
         hello(at_x(k))
-    pl.semaphore_wait(barrier, 25)
+    pl.semaphore_wait(barrier, 10)
+
+    def spread(turn):
+        if turn > 0:
+            for way in range(4):
+                pl.semaphore_wait(known.at[way], 1)
+        if turn < 3:
+            for way, device in enumerate((at_z(1), at_z(-1), at_y(1, c), at_y(-1, c))):
+                pl.semaphore_signal(known.at[way], inc=1, device_id=device, device_id_type=MESH)
 
     def part(i):
         return pl.ds(pl.multiple_of(i * CH, CH), CH)
@@ -141,16 +150,13 @@
             if k < 3:
                 z_relay(UP[k], UP[k + 1], i, True).start()
             else:
-                @pl.when(i < NCH // 2)
-                def _():
+                if i < NCH // 2:
                     z_relay(UP[3], UP[4], i, True).start()
             landed(raw.at[DOWN[k], part(i)], z_recv.at[DOWN[k] - 5, i])
             if k < 3:
                 z_relay(DOWN[k], DOWN[k + 1], i, False).start()
-            else:
-                @pl.when(i >= NCH // 2)
-                def _():
-                    z_relay(DOWN[3], UP[4], i, False).start()
+            elif i >= NCH // 2:
+                z_relay(DOWN[3], UP[4], i, False).start()
         else:
             landed(raw.at[UP[4], part(i)], z_recv.at[UP[4] - 5, i])
 
@@ -172,6 +178,8 @@
             y_own_partner(i).start()
         each(go)
 
+    spread(0)
+
     sums = jnp.sum(x_ref[...], axis=0, keepdims=True)
     zs[z] = jnp.zeros((8, LANES), jnp.float32)
     for k in range(COLS):
@@ -180,51 +188,50 @@
     def ms_copy(k):
         return remote(zs.at[z], zs.at[z], ms_send.at[k - 1], ms_recv.at[k - 1], at_z(k))
 
-    for k in range(1, 8):
-        ms_copy(k).start()
-
-    def phase_one(dist):
-        def step(i):
-            y_event(dist, i)
+    mine = 2 * a + c
+
+    def mt_copy(k):
+        return remote(zt, ys.at[mine], mt_send.at[k], mt_recv.at[mine], at_y(k, h))
+
+    def sums_over_z():
+        for k in range(1, 8):
+            source = rem(z + 8 - k, 8)
+            landed(zs.at[source], ms_recv.at[k - 1])
+        total = zs[0]
+        for k in range(1, 8):
+            total = total + zs[k]
+        zt[...] = total
+        for k in range(1, 8):
+            mt_copy(k).start()
+
+        @pl.when(first)
+        def _():
+            ys[mine] = total
+
+        @pl.when(other)
+        def _():
+            mt_copy(0).start()
+
+    for k in range(1, 5):
+        for i in range(NCH):
+            y_event(k, i)
 
             @pl.when(first)
             def _():
-                z_event(dist, i)
-
-            if dist == 4:
+                z_event(k, i)
+
+            if k == 4:
                 @pl.when(other)
                 def _():
                     z_start(raw.at[0], i, True).start()
                     z_start(raw.at[0], i, False).start()
-        each(step)
-
-    phase_one(1)
-
-    mine = 2 * a + c
-
-    def mt_copy(k):
-        return remote(zt, ys.at[mine], mt_send.at[k], mt_recv.at[mine], at_y(k, h))
-
-    for k in range(1, 8):
-        source = rem(z + 8 - k, 8)
-        landed(zs.at[source], ms_recv.at[k - 1])
-    total = zs[0]
-    for k in range(1, 8):
-        total = total + zs[k]
-    zt[...] = total
-    for k in range(1, 8):
-        mt_copy(k).start()
-
-    @pl.when(first)
-    def _():
-        ys[mine] = total
-
-    @pl.when(other)
-    def _():
-        mt_copy(0).start()
-
-    for dist in range(2, 5):
-        phase_one(dist)
+            if k == 1 and i < 3:
+                spread(i + 1)
+            if k == 1 and i == 2:
+                for j in range(1, 8):
+                    ms_copy(j).start()
+        if k == SUMS_AT:
+            sums_over_z()
 
     @pl.when(first)
     def _():
@@ -247,8 +254,6 @@
         top = value.astype(jnp.bfloat16)
         hi[slot] = top
         lo[slot] = (value - top.astype(jnp.float32)).astype(jnp.bfloat16)
-
-    lax.fori_loop(0, 5, lambda s, _: (convert(s), 0)[1], 0)
 
     e_mine = y
 
@@ -291,27 +296,25 @@
         for xx in range(4):
             for yy in range(2):
                 start = 32 * xx + 16 * yy
-                pk[yy, xx, index] = acc[start : start + 16, :]
+                pk[xx, index, yy] = acc[start : start + 16, :]
 
     def d_copy(k):
         t0, n = GROUPS[k]
-        return remote(
-            pk.at[1 - c, :, pl.ds(t0, n)], pr.at[:, pl.ds(t0, n)], d_send.at[k], d_recv.at[k], partner
-        )
+        tiles = pl.ds(t0, n)
+        return remote(pk.at[:, tiles], pr.at[:, tiles], d_send.at[k], d_recv.at[k], partner)
 
     def x_copy(k, s):
         t0, n = GROUPS[k]
         return remote(
-            sx.at[rem(x + s, 4), pl.ds(t0, n)], xr.at[s - 1, pl.ds(t0, n)],
+            pk.at[rem(x + s, 4), pl.ds(t0, n)], xr.at[s - 1, pl.ds(t0, n)],
             x_send.at[k, s - 1], x_recv.at[k, s - 1], at_x(s),
         )
 
     def over_cores(k):
         t0, n = GROUPS[k]
-        landed(pr.at[:, pl.ds(t0, n)], d_recv.at[k])
-        sx[:, t0 : t0 + n] = pk[c, :, t0 : t0 + n] + pr[:, t0 : t0 + n]
-        for s in range(1, 4):
-            x_copy(k, s).start()
+        tiles = pl.ds(t0, n)
+        landed(pr.at[:, tiles], d_recv.at[k])
+        pk[:, tiles] = pk[:, tiles] + pr[:, tiles]
 
     def target(k, t):
         r, j, swap = tile_of(k, t)
@@ -326,75 +329,128 @@
         a_row = jnp.where(swap, a, a_row)
         z_row = jnp.where(swap, z, z_row)
         c_row = jnp.where(swap, h, c_row)
-        local = (a_row == a) & (z_row == z) & (c_row == c) & (c == h)
-        return valid, local, (a_row, z_row, c_row, x, c), d
-
-    def f_copy(k, t):
-        _, _, device, d = target(k, t)
+        mine = (a_row == a) & (z_row == z) & (c_row == c)
+        return valid, mine, (a_row, z_row, c_row), d
+
+    def f_copy(k, t, row, d, hh):
         index = GROUPS[k][0] + t
-        return remote(fb.at[index], out_ref.at[0, d], f_send.at[index], f_recv.at[d], device)
+        return remote(
+            fb.at[index, hh], out_ref.at[0, d], f_send.at[index, hh], f_recv.at[d], (*row, x, hh)
+        )
+
+    def g_copy(t, row, d, xx, hh):
+        return remote(
+            pk.at[xx, GROUPS[4][0] + t, hh], home.at[x, d],
+            g_send.at[t, xx, hh], g_recv.at[x, d], (*row, xx, hh),
+        )
 
     def over_planes(k):
         t0, n = GROUPS[k]
         for s in range(1, 4):
             landed(xr.at[s - 1, pl.ds(t0, n)], x_recv.at[k, s - 1])
-        block = pl.ds(t0, n)
-        fb[block] = (sx[x, block] + xr[0, block] + xr[1, block] + xr[2, block]) * (1.0 / NPARAMS)
+        tiles = pl.ds(t0, n)
+        fb[tiles] = (pk[x, tiles] + xr[0, tiles] + xr[1, tiles] + xr[2, tiles]) * (1.0 / NPARAMS)
 
         def send(t, carry):
-            valid, local, _, d = target(k, t)
-
-            @pl.when(jnp.logical_and(valid, local))
-            def _():
-                out_ref[0, d] = fb[t0 + t]
-
-            @pl.when(jnp.logical_and(valid, jnp.logical_not(local)))
-            def _():
-                f_copy(k, t).start()
+            valid, mine, row, d = target(k, t)
+            for hh in range(2):
+                local = mine & (h == hh)
+
+                @pl.when(jnp.logical_and(valid, local))
+                def _():
+                    out_ref[0, d] = fb[t0 + t, hh]
+
+                @pl.when(jnp.logical_and(valid, jnp.logical_not(local)))
+                def _():
+                    f_copy(k, t, row, d, hh).start()
 
             return carry
 
         lax.fori_loop(0, n, send, 0)
 
+    def go_home():
+        def send(t, carry):
+            valid, mine, row, d = target(4, t)
+            for xx in range(4):
+                for hh in range(2):
+                    local = mine & (h == hh) & (x == xx)
+
+                    @pl.when(jnp.logical_and(valid, local))
+                    def _():
+                        home[xx, d] = pk[xx, GROUPS[4][0] + t, hh]
+
+                    @pl.when(jnp.logical_and(valid, jnp.logical_not(local)))
+                    def _():
+                        g_copy(t, row, d, xx, hh).start()
+
+            return carry
+
+        lax.fori_loop(0, GROUPS[4][1], send, 0)
+
+    def some(k, start, stop):
+        lax.fori_loop(start, stop, lambda t, _: (compute(k, t), 0)[1], 0)
+
+    def arrives(k, i):
+        @pl.when(other)
+        def _():
+            z_event(k, i)
+
     for k in range(5):
-        if 1 <= k <= 3:
+        n = GROUPS[k][1]
+        if k < 4:
+            arrives(k + 1, 0)
+        if k == 0:
+            lax.fori_loop(0, 5, lambda s, _: (convert(s), 0)[1], 0)
+        elif k < 4:
             convert(UP[k])
             convert(DOWN[k])
-        if k == 4:
+        else:
             convert(UP[4])
-        n = GROUPS[k][1]
-        per = -(-n // NCH)
-
-        def step(i):
+        some(k, 0, n // 2)
+        if k < 4:
+            arrives(k + 1, 1)
+        some(k, n // 2, n)
+
+        @pl.when(first)
+        def _():
+            d_copy(k).start()
+
+        @pl.when(other)
+        def _():
             if k < 4:
-                @pl.when(other)
+                z_event(k + 1, 2)
+            over_cores(k)
+            if k < 4:
+                for s in range(1, 4):
+                    x_copy(k, s).start()
+                z_event(k + 1, 3)
+            else:
+                go_home()
+            if k:
+                over_planes(k - 1)
+
+    def arrived(d, carry):
+        local = d < 0
+        for j in range(5):
+            gap = rem(2 * (rem(z + j, 8) - z) + h - c + NB, NB)
+            here = d == gap
+            if j == 0:
+                here = here & (h == 0)
+            if j == 4:
+                here = here & (h == 1)
+            local = local | here
+        local = local & other
+        last = rem(div(rem(16 * a + 2 * z + c + d, NB), 2) + 8 - z, 8) == 4
+
+        @pl.when(last)
+        def _():
+            for xx in range(4):
+                @pl.when(jnp.logical_not(local & (x == xx)))
                 def _():
-                    z_event(k + 1, i)
-            for u in range(per):
-                if per * NCH <= n:
-                    compute(k, i * per + u)
-                else:
-                    @pl.when(i * per + u < n)
-                    def _():
-                        compute(k, i * per + u)
-
-        each(step)
-        d_copy(k).start()
-        over_cores(k)
-        if k:
-            over_planes(k - 1)
-    over_planes(4)
-
-    def arrived(d, carry):
-        step = div(d, 2)
-        local = (rem(d, 2) == 0) & (step <= 4) & (z + step <= 7)
-        for r in range(1, 5):
-            _, gap, _, _ = pair(r, 0)
-            here = (gap >= HALF) & (d == NB - gap)
-            local = local | ((here & (h == 0)) if r == 4 else here)
-        local = local & first
-
-        @pl.when(jnp.logical_not(local))
+                    landed(home.at[xx, d], g_recv.at[xx, d])
+            out_ref[0, d] = (home[0, d] + home[1, d] + home[2, d] + home[3, d]) * (1.0 / NPARAMS)
+
+        @pl.when(jnp.logical_not(last | local))
         def _():
             landed(out_ref.at[0, d], f_recv.at[d])
 
@@ -439,25 +495,38 @@
         ms_copy(k).wait_send()
         mt_copy(k).wait_send()
 
+    @pl.when(first)
+    def _():
+        for k in range(5):
+            d_copy(k).wait_send()
+
     @pl.when(other)
     def _():
         mt_copy(0).wait_send()
-
-    for k in range(5):
-        d_copy(k).wait_send()
-        for s in range(1, 4):
-            x_copy(k, s).wait_send()
-
-        def gone(t, carry):
-            valid, local, _, _ = target(k, t)
-
-            @pl.when(jnp.logical_and(valid, jnp.logical_not(local)))
-            def _():
-                f_copy(k, t).wait_send()
-
+        for k in range(4):
+            for s in range(1, 4):
+                x_copy(k, s).wait_send()
+
+            def gone(t, carry):
+                valid, mine, row, d = target(k, t)
+                for hh in range(2):
+                    @pl.when(jnp.logical_and(valid, jnp.logical_not(mine & (h == hh))))
+                    def _():
+                        f_copy(k, t, row, d, hh).wait_send()
+                return carry
+
+            lax.fori_loop(0, GROUPS[k][1], gone, 0)
+
+        def left(t, carry):
+            valid, mine, row, d = target(4, t)
+            for xx in range(4):
+                for hh in range(2):
+                    @pl.when(jnp.logical_and(valid, jnp.logical_not(mine & (h == hh) & (x == xx))))
+                    def _():
+                        g_copy(t, row, d, xx, hh).wait_send()
             return carry
 
-        lax.fori_loop(0, GROUPS[k][1], gone, 0)
+        lax.fori_loop(0, GROUPS[4][1], left, 0)
 
 
 def on_device(logder):
@@ -476,11 +545,11 @@
             pltpu.VMEM((8, LANES), f32),
             pltpu.VMEM((8, 8, LANES), f32),
             pltpu.VMEM((8, LANES), f32),
-            pltpu.VMEM((2, 4, NTILE, 16, ROWS), f32),
-            pltpu.VMEM((4, NTILE, 16, ROWS), f32),
-            pltpu.VMEM((4, NTILE, 16, ROWS), f32),
-            pltpu.VMEM((3, NTILE, 16, ROWS), f32),
-            pltpu.VMEM((NTILE, 16, ROWS), f32),
+            pltpu.VMEM((4, NTILE, 2, 16, ROWS), f32),
+            pltpu.VMEM((4, NTILE, 2, 16, ROWS), f32),
+            pltpu.VMEM((3, NTILE, 2, 16, ROWS), f32),
+            pltpu.VMEM((NTILE, 2, 16, ROWS), f32),
+            pltpu.VMEM((4, HALF + 1, 16, ROWS), f32),
             dma((2, NCH)),
             dma((5, NCH)),
             dma((5, NCH)),
@@ -491,12 +560,15 @@
             dma((7,)),
             dma((8,)),
             dma((8,)),
+            pltpu.SemaphoreType.REGULAR((4,)),
             dma((5,)),
             dma((5,)),
             dma((5, 3)),
             dma((5, 3)),
-            dma((NTILE,)),
+            dma((NTILE, 2)),
             dma((HALF + 1,)),
+            dma((5, 4, 2)),
+            dma((4, HALF + 1)),
         ],
         compiler_params=pltpu.CompilerParams(collective_id=0, has_side_effects=True),
     )(logder)

time: 80.1 us -> 76.5 us (0.955)
  Pallas kernels: 78.2 us -> 74.7 us
    pallas_call x1, Pallas kernels: 78.2 us -> 74.7 us  [on_device(): pl.pallas_call(kernel, out_shape=jax.ShapeDtypeStruct((1, HALF + 1, 16, R...]
where the time goes in v2:
time: 76.5 us; the launch traced here: 76.4 us
  Pallas kernels  74.7 us (98%)
  local copies, waits for them, and re-layouts  1.68 us (2%)
    pallas_call x1, Pallas kernels, on_device(): pl.pallas_call(kernel, out_shape=jax.ShapeDtypeStruct((1, HALF + 1, 16, R...  74.7 us
    unnamed x1, local copies, waits for them, and re-layouts  1.68 us

profile of v2, /device:TPU:1, one launch (start us, length us, event | category | flops | bytes accessed | tf_op | source)
XLA Modules:
  0.0 76.4 jit_solution(14644094223886295676)
XLA Ops:
  0.0 74.7 %shard_map.17 = f32[1,33,16,128]{3,2,1,0:T(8,128)} custom-call(f32[128,768]{1,0:T(8,128)} %x_ref.1), custom_call_target="tpu_custom_call" | custom-call | tf_op jit(solution)/shard_map/pallas_call | solution.py:535
  74.7 1.7 %copy.3 = f32[1,33,16,128]{3,2,1,0:T(8,128)} copy(f32[1,33,16,128]{3,2,1,0:T(8,128)} %shard_map.17) | data formatting | bytes 540672

commit v3 on v2

--- a/solution.py
+++ b/solution.py
@@ -36,7 +36,7 @@
 
 
 def kernel(
-    x_ref, out_ref, raw, hi, lo, zs, zt, ys, mean, pk, pr, xr, fb, home,
+    x_ref, out_ref, raw, hl, zs, zt, ys, mean, pk, pr, xr, fb, home,
     own_send, y_send, y_recv, z_send, z_own, z_recv, ms_send, ms_recv, mt_send, mt_recv,
     known, d_send, d_recv, x_send, x_recv, f_send, f_recv, g_send, g_recv,
 ):
@@ -99,33 +99,33 @@
         return div(rem(y + 8 - r, 8), 4) == c
 
     def y_own_up(i):
-        return remote(x_ref.at[part(i)], raw.at[1, part(i)], own_send.at[0, i], y_recv.at[1, i], at_y(1, c))
+        return remote(x_ref.at[part(i)], raw.at[1, part(i)], own_send.at[0], y_recv.at[1, i], at_y(1, c))
 
     def y_own_down(i):
         return remote(
-            x_ref.at[part(i)], raw.at[3, part(i)], own_send.at[0, i], y_recv.at[3, i], at_y(-1, 1 - c)
+            x_ref.at[part(i)], raw.at[3, part(i)], own_send.at[0], y_recv.at[3, i], at_y(-1, 1 - c)
         )
 
     def y_own_partner(i):
-        return remote(x_ref.at[part(i)], raw.at[4, part(i)], own_send.at[1, i], y_recv.at[4, i], partner)
+        return remote(x_ref.at[part(i)], raw.at[4, part(i)], own_send.at[1], y_recv.at[4, i], partner)
 
     def y_relay(r, up, i):
         to = r + 1 if up else r - 1
         return remote(
-            raw.at[r, part(i)], raw.at[to, part(i)], y_send.at[r, i], y_recv.at[to, i],
+            raw.at[r, part(i)], raw.at[to, part(i)], y_send.at[r], y_recv.at[to, i],
             at_y(1 if up else -1, c),
         )
 
     def z_start(src, i, low):
         to = UP[1] if low else DOWN[1]
         return remote(
-            src.at[part(i)], raw.at[to, part(i)], z_own.at[0 if low else 1, i], z_recv.at[to - 5, i],
+            src.at[part(i)], raw.at[to, part(i)], z_own.at[0 if low else 1], z_recv.at[to - 5, i],
             at_z(-1 if low else 1),
         )
 
     def z_relay(slot, to, i, low):
         return remote(
-            raw.at[slot, part(i)], raw.at[to, part(i)], z_send.at[slot - 5, i], z_recv.at[to - 5, i],
+            raw.at[slot, part(i)], raw.at[to, part(i)], z_send.at[slot - 5], z_recv.at[to - 5, i],
             at_z(-1 if low else 1),
         )
 
@@ -186,17 +186,15 @@
         zs[z, k : k + 1, :] = sums[:, k * LANES : (k + 1) * LANES]
 
     def ms_copy(k):
-        return remote(zs.at[z], zs.at[z], ms_send.at[k - 1], ms_recv.at[k - 1], at_z(k))
+        return remote(zs.at[z], zs.at[z], ms_send, ms_recv, at_z(k))
 
     mine = 2 * a + c
 
     def mt_copy(k):
-        return remote(zt, ys.at[mine], mt_send.at[k], mt_recv.at[mine], at_y(k, h))
+        return remote(zt, ys.at[mine], mt_send, mt_recv, at_y(k, h))
 
     def sums_over_z():
-        for k in range(1, 8):
-            source = rem(z + 8 - k, 8)
-            landed(zs.at[source], ms_recv.at[k - 1])
+        landed(zs.at[pl.ds(0, 7)], ms_recv)
         total = zs[0]
         for k in range(1, 8):
             total = total + zs[k]
@@ -216,11 +214,11 @@
         for i in range(NCH):
             y_event(k, i)
 
-            @pl.when(first)
-            def _():
-                z_event(k, i)
-
-            if k == 4:
+            if k < 4:
+                @pl.when(first)
+                def _():
+                    z_event(k, i)
+            else:
                 @pl.when(other)
                 def _():
                     z_start(raw.at[0], i, True).start()
@@ -238,22 +236,27 @@
         each(lambda i: landed(raw.at[4, part(i)], y_recv.at[4, i]))
         raw[0] = x_ref[...]
 
-    for k in range(8):
-        @pl.when(jnp.logical_or(other, mine != k))
+    def wait_mean():
+        @pl.when(first)
         def _():
-            landed(ys.at[k], mt_recv.at[k])
-    total = ys[0]
-    for k in range(1, 8):
-        total = total + ys[k]
-    mean[...] = total * (1.0 / NSAMPLES)
+            landed(ys.at[pl.ds(0, 7)], mt_recv)
+
+        @pl.when(other)
+        def _():
+            landed(ys, mt_recv)
+
+        total = ys[0]
+        for k in range(1, 8):
+            total = total + ys[k]
+        mean[...] = total * (1.0 / NSAMPLES)
 
     def convert(slot):
         m = mean[...]
         row = jnp.concatenate([m[k : k + 1, :] for k in range(COLS)], axis=1)
         value = raw[slot] - row
         top = value.astype(jnp.bfloat16)
-        hi[slot] = top
-        lo[slot] = (value - top.astype(jnp.float32)).astype(jnp.bfloat16)
+        hl[slot, :ROWS] = top
+        hl[slot, ROWS:] = (value - top.astype(jnp.float32)).astype(jnp.bfloat16)
 
     e_mine = y
 
@@ -291,7 +294,8 @@
         keep = jnp.logical_xor(keep, swap)
         row = jnp.where(keep, r, slot_of(j))
         col = jnp.where(keep, slot_of(j), r)
-        acc = dot(hi[row], hi[col]) + dot(hi[row], lo[col]) + dot(lo[row], hi[col])
+        both = dot(hl[row], hl[col, :ROWS])
+        acc = both[:ROWS] + both[ROWS:] + dot(hl[row, :ROWS], hl[col, ROWS:])
         index = GROUPS[k][0] + t
         for xx in range(4):
             for yy in range(2):
@@ -307,7 +311,7 @@
         t0, n = GROUPS[k]
         return remote(
             pk.at[rem(x + s, 4), pl.ds(t0, n)], xr.at[s - 1, pl.ds(t0, n)],
-            x_send.at[k, s - 1], x_recv.at[k, s - 1], at_x(s),
+            x_send.at[k], x_recv.at[k], at_x(s),
         )
 
     def over_cores(k):
@@ -335,20 +339,20 @@
     def f_copy(k, t, row, d, hh):
         index = GROUPS[k][0] + t
         return remote(
-            fb.at[index, hh], out_ref.at[0, d], f_send.at[index, hh], f_recv.at[d], (*row, x, hh)
+            fb.at[index, hh], out_ref.at[0, d], f_send.at[index], f_recv.at[d], (*row, x, hh)
         )
 
     def g_copy(t, row, d, xx, hh):
+        place = 2 * div(d, 16) + rem(row[2] + d, 2)
         return remote(
-            pk.at[xx, GROUPS[4][0] + t, hh], home.at[x, d],
-            g_send.at[t, xx, hh], g_recv.at[x, d], (*row, xx, hh),
+            pk.at[xx, GROUPS[4][0] + t, hh], home.at[x, place],
+            g_send.at[t], g_recv.at[x, place], (*row, xx, hh),
         )
 
     def over_planes(k):
         t0, n = GROUPS[k]
-        for s in range(1, 4):
-            landed(xr.at[s - 1, pl.ds(t0, n)], x_recv.at[k, s - 1])
         tiles = pl.ds(t0, n)
+        landed(xr.at[:, tiles], x_recv.at[k])
         fb[tiles] = (pk[x, tiles] + xr[0, tiles] + xr[1, tiles] + xr[2, tiles]) * (1.0 / NPARAMS)
 
         def send(t, carry):
@@ -377,7 +381,7 @@
 
                     @pl.when(jnp.logical_and(valid, local))
                     def _():
-                        home[xx, d] = pk[xx, GROUPS[4][0] + t, hh]
+                        home[xx, 2 * div(d, 16) + rem(row[2] + d, 2)] = pk[xx, GROUPS[4][0] + t, hh]
 
                     @pl.when(jnp.logical_and(valid, jnp.logical_not(local)))
                     def _():
@@ -390,65 +394,139 @@
     def some(k, start, stop):
         lax.fori_loop(start, stop, lambda t, _: (compute(k, t), 0)[1], 0)
 
-    def arrives(k, i):
-        @pl.when(other)
-        def _():
-            z_event(k, i)
-
-    for k in range(5):
-        n = GROUPS[k][1]
-        if k < 4:
-            arrives(k + 1, 0)
+    def convert_round(k):
         if k == 0:
+            wait_mean()
             lax.fori_loop(0, 5, lambda s, _: (convert(s), 0)[1], 0)
         elif k < 4:
             convert(UP[k])
             convert(DOWN[k])
         else:
             convert(UP[4])
-        some(k, 0, n // 2)
+
+    @pl.when(other)
+    def _():
+        for k in range(5):
+            n = GROUPS[k][1]
+            if k < 4:
+                z_event(k + 1, 0)
+            if k == 0:
+                z_event(1, 1)
+            convert_round(k)
+            if k == 0:
+                z_event(1, 2)
+            elif k < 4:
+                z_event(k + 1, 1)
+            some(k, 0, n // 2)
+            if k == 0:
+                z_event(1, 3)
+            elif k < 4:
+                z_event(k + 1, 2)
+            some(k, n // 2, n)
+            d_copy(k).start()
+            if 0 < k < 4:
+                z_event(k + 1, 3)
+
+    def plane_sums(k):
+        over_cores(k)
         if k < 4:
-            arrives(k + 1, 1)
-        some(k, n // 2, n)
-
-        @pl.when(first)
-        def _():
-            d_copy(k).start()
-
-        @pl.when(other)
-        def _():
-            if k < 4:
-                z_event(k + 1, 2)
-            over_cores(k)
-            if k < 4:
-                for s in range(1, 4):
-                    x_copy(k, s).start()
-                z_event(k + 1, 3)
-            else:
-                go_home()
-            if k:
-                over_planes(k - 1)
+            for s in range(1, 4):
+                x_copy(k, s).start()
+        else:
+            go_home()
+
+    @pl.when(first)
+    def _():
+        for k in range(5):
+            if k == 4:
+                for i in range(NCH):
+                    z_event(4, i)
+            convert_round(k)
+            some(k, 0, GROUPS[k][1])
+            if k == 3:
+                plane_sums(0)
+        for k in range(1, 5):
+            plane_sums(k)
+            if k > 1:
+                over_planes(k - 2)
+        over_planes(3)
+
+    @pl.when(first)
+    def _():
+        remote(x_ref, raw.at[1], own_send.at[0], y_recv.at[1, 0], at_y(1, c)).wait_send()
+
+    @pl.when(other)
+    def _():
+        for k in range(2):
+            remote(x_ref, raw.at[3], own_send.at[k], y_recv.at[3, 0], partner).wait_send()
+
+    for k in range(2):
+        remote(x_ref, raw.at[5], z_own.at[k], z_recv.at[0, 0], at_z(1)).wait_send()
+    for r in range(1, 4):
+        remote(raw.at[r], raw.at[r], y_send.at[r], y_recv.at[r, 0], at_z(1)).wait_send()
+    for k in range(1, 4):
+        for slot in (UP[k], DOWN[k]):
+            piece = raw.at[slot] if k < 3 else raw.at[slot, pl.ds(0, ROWS // 2)]
+            remote(piece, piece, z_send.at[slot - 5], z_recv.at[slot - 5, 0], at_z(1)).wait_send()
+    remote(zs.at[pl.ds(0, 7)], zs.at[pl.ds(0, 7)], ms_send, ms_recv, at_z(1)).wait_send()
+
+    @pl.when(first)
+    def _():
+        remote(ys.at[pl.ds(0, 7)], ys.at[pl.ds(0, 7)], mt_send, mt_recv, at_z(1)).wait_send()
+        for k in range(4):
+            t0, n = GROUPS[k]
+            tiles = xr.at[:, pl.ds(t0, n)]
+            remote(tiles, tiles, x_send.at[k], x_recv.at[k], at_z(1)).wait_send()
+
+            def gone(t, carry):
+                valid, mine, _, _ = target(k, t)
+
+                @pl.when(valid & mine)
+                def _():
+                    piece = fb.at[0, 0]
+                    remote(piece, piece, f_send.at[t0 + t], f_recv.at[0], at_z(1)).wait_send()
+
+                @pl.when(valid & jnp.logical_not(mine))
+                def _():
+                    pieces = fb.at[0]
+                    remote(pieces, pieces, f_send.at[t0 + t], f_recv.at[0], at_z(1)).wait_send()
+
+                return carry
+
+            lax.fori_loop(0, n, gone, 0)
+
+        def left(t, carry):
+            valid, mine, _, _ = target(4, t)
+
+            @pl.when(valid & mine)
+            def _():
+                pieces = pk.at[0, pl.ds(0, 7), 0]
+                remote(pieces, pieces, g_send.at[t], g_recv.at[0, 0], at_z(1)).wait_send()
+
+            @pl.when(valid & jnp.logical_not(mine))
+            def _():
+                pieces = pk.at[0, pl.ds(0, 8), 0]
+                remote(pieces, pieces, g_send.at[t], g_recv.at[0, 0], at_z(1)).wait_send()
+
+            return carry
+
+        lax.fori_loop(0, GROUPS[4][1], left, 0)
+
+    @pl.when(other)
+    def _():
+        remote(ys, ys, mt_send, mt_recv, at_z(1)).wait_send()
+        for k in range(5):
+            d_copy(k).wait_send()
 
     def arrived(d, carry):
-        local = d < 0
-        for j in range(5):
-            gap = rem(2 * (rem(z + j, 8) - z) + h - c + NB, NB)
-            here = d == gap
-            if j == 0:
-                here = here & (h == 0)
-            if j == 4:
-                here = here & (h == 1)
-            local = local | here
-        local = local & other
+        step = div(d, 2)
+        local = (rem(d, 2) == 0) & (step <= 4) & (z + step <= 7)
+        for r in range(1, 5):
+            _, gap, _, _ = pair(r, 0)
+            here = (gap >= HALF) & (d == NB - gap)
+            local = local | ((here & (h == 0)) if r == 4 else here)
+        local = local & first
         last = rem(div(rem(16 * a + 2 * z + c + d, NB), 2) + 8 - z, 8) == 4
-
-        @pl.when(last)
-        def _():
-            for xx in range(4):
-                @pl.when(jnp.logical_not(local & (x == xx)))
-                def _():
-                    landed(home.at[xx, d], g_recv.at[xx, d])
-            out_ref[0, d] = (home[0, d] + home[1, d] + home[2, d] + home[3, d]) * (1.0 / NPARAMS)
 
         @pl.when(jnp.logical_not(last | local))
         def _():
@@ -458,75 +536,14 @@
 
     lax.fori_loop(0, HALF + 1, arrived, 0)
 
-    def sent(i):
-        @pl.when(first)
-        def _():
-            y_own_up(i).wait_send()
-
-        @pl.when(other)
-        def _():
-            y_own_down(i).wait_send()
-            y_own_partner(i).wait_send()
-
-        z_start(x_ref, i, True).wait_send()
-        z_start(x_ref, i, False).wait_send()
-        for dist in range(1, 4):
-            @pl.when(from_below(dist))
+    for place in range(4):
+        d = 16 * (place // 2) + 8 + (place % 2) - c
+        for xx in range(4):
+            @pl.when(jnp.logical_not(first & (d == 8) & (z < 4) & (x == xx)))
             def _():
-                y_relay(dist, True, i).wait_send()
-
-            @pl.when(jnp.logical_not(from_below(4 - dist)))
-            def _():
-                y_relay(4 - dist, False, i).wait_send()
-        for k in range(1, 3):
-            z_relay(UP[k], UP[k + 1], i, True).wait_send()
-            z_relay(DOWN[k], DOWN[k + 1], i, False).wait_send()
-
-        @pl.when(i < NCH // 2)
-        def _():
-            z_relay(UP[3], UP[4], i, True).wait_send()
-
-        @pl.when(i >= NCH // 2)
-        def _():
-            z_relay(DOWN[3], UP[4], i, False).wait_send()
-
-    each(sent)
-    for k in range(1, 8):
-        ms_copy(k).wait_send()
-        mt_copy(k).wait_send()
-
-    @pl.when(first)
-    def _():
-        for k in range(5):
-            d_copy(k).wait_send()
-
-    @pl.when(other)
-    def _():
-        mt_copy(0).wait_send()
-        for k in range(4):
-            for s in range(1, 4):
-                x_copy(k, s).wait_send()
-
-            def gone(t, carry):
-                valid, mine, row, d = target(k, t)
-                for hh in range(2):
-                    @pl.when(jnp.logical_and(valid, jnp.logical_not(mine & (h == hh))))
-                    def _():
-                        f_copy(k, t, row, d, hh).wait_send()
-                return carry
-
-            lax.fori_loop(0, GROUPS[k][1], gone, 0)
-
-        def left(t, carry):
-            valid, mine, row, d = target(4, t)
-            for xx in range(4):
-                for hh in range(2):
-                    @pl.when(jnp.logical_and(valid, jnp.logical_not(mine & (h == hh) & (x == xx))))
-                    def _():
-                        g_copy(t, row, d, xx, hh).wait_send()
-            return carry
-
-        lax.fori_loop(0, GROUPS[4][1], left, 0)
+                landed(home.at[xx, place], g_recv.at[xx, place])
+        total = home[0, place] + home[1, place] + home[2, place] + home[3, place]
+        out_ref[0, d] = total * (1.0 / NPARAMS)
 
 
 def on_device(logder):
@@ -539,8 +556,7 @@
         out_specs=pl.BlockSpec(memory_space=pltpu.VMEM),
         scratch_shapes=[
             pltpu.VMEM((NSLOT, ROWS, WIDTH), f32),
-            pltpu.VMEM((NSLOT, ROWS, WIDTH), bf16),
-            pltpu.VMEM((NSLOT, ROWS, WIDTH), bf16),
+            pltpu.VMEM((NSLOT, 2 * ROWS, WIDTH), bf16),
             pltpu.VMEM((8, 8, LANES), f32),
             pltpu.VMEM((8, LANES), f32),
             pltpu.VMEM((8, 8, LANES), f32),
@@ -549,26 +565,26 @@
             pltpu.VMEM((4, NTILE, 2, 16, ROWS), f32),
             pltpu.VMEM((3, NTILE, 2, 16, ROWS), f32),
             pltpu.VMEM((NTILE, 2, 16, ROWS), f32),
-            pltpu.VMEM((4, HALF + 1, 16, ROWS), f32),
-            dma((2, NCH)),
+            pltpu.VMEM((4, 4, 16, ROWS), f32),
+            dma((2,)),
+            dma((5,)),
             dma((5, NCH)),
-            dma((5, NCH)),
+            dma((7,)),
+            dma((2,)),
             dma((7, NCH)),
-            dma((2, NCH)),
-            dma((7, NCH)),
-            dma((7,)),
-            dma((7,)),
-            dma((8,)),
-            dma((8,)),
+            dma(()),
+            dma(()),
+            dma(()),
+            dma(()),
             pltpu.SemaphoreType.REGULAR((4,)),
             dma((5,)),
             dma((5,)),
-            dma((5, 3)),
-            dma((5, 3)),
-            dma((NTILE, 2)),
+            dma((4,)),
+            dma((4,)),
+            dma((NTILE,)),
             dma((HALF + 1,)),
-            dma((5, 4, 2)),
-            dma((4, HALF + 1)),
+            dma((5,)),
+            dma((4, 4)),
         ],
         compiler_params=pltpu.CompilerParams(collective_id=0, has_side_effects=True),
     )(logder)

time: 76.5 us -> 72.8 us (0.952)
  Pallas kernels: 74.7 us -> 70.9 us
    pallas_call x1, Pallas kernels: 74.7 us -> 70.9 us  [on_device(): pl.pallas_call(kernel, out_shape=jax.ShapeDtypeStruct((1, HALF + 1, 16, R...]
where the time goes in v3:
time: 72.8 us; the launch traced here: 72.6 us
  Pallas kernels  70.9 us (97%)
  local copies, waits for them, and re-layouts  1.68 us (2%)
    pallas_call x1, Pallas kernels, on_device(): pl.pallas_call(kernel, out_shape=jax.ShapeDtypeStruct((1, HALF + 1, 16, R...  70.9 us
    unnamed x1, local copies, waits for them, and re-layouts  1.68 us

profile of v3, /device:TPU:1, one launch (start us, length us, event | category | flops | bytes accessed | tf_op | source)
XLA Modules:
  0.0 72.6 jit_solution(1614442032768528069)
XLA Ops:
  0.0 70.9 %shard_map.17 = f32[1,33,16,128]{3,2,1,0:T(8,128)} custom-call(f32[128,768]{1,0:T(8,128)} %x_ref.1), custom_call_target="tpu_custom_call" | custom-call | tf_op jit(solution)/shard_map/pallas_call | solution.py:552
  71.0 1.7 %copy.3 = f32[1,33,16,128]{3,2,1,0:T(8,128)} copy(f32[1,33,16,128]{3,2,1,0:T(8,128)} %shard_map.17) | data formatting | bytes 540672

commit v4 on v3

--- a/solution.py
+++ b/solution.py
@@ -36,9 +36,9 @@
 
 
 def kernel(
-    x_ref, out_ref, raw, hl, zs, zt, ys, mean, pk, pr, xr, fb, home,
+    x_hbm, out_ref, x_ref, raw, hl, zs, zt, ys, mean, pk, pr, xr, fb, home,
     own_send, y_send, y_recv, z_send, z_own, z_recv, ms_send, ms_recv, mt_send, mt_recv,
-    known, d_send, d_recv, x_send, x_recv, f_send, f_recv, g_send, g_recv,
+    known, x_in, d_send, d_recv, x_send, x_recv, f_send, f_recv, g_send, g_recv,
 ):
     a = lax.axis_index("a")
     z = lax.axis_index("z")
@@ -70,6 +70,9 @@
     def landed(ref, sem):
         pltpu.make_async_copy(ref, ref, sem).wait()
 
+    fetch = pltpu.make_async_copy(x_hbm, x_ref, x_in)
+    fetch.start()
+
     barrier = pltpu.get_barrier_semaphore()
 
     def hello(device):
@@ -83,6 +86,7 @@
     for k in range(1, 4):
         hello(at_x(k))
     pl.semaphore_wait(barrier, 10)
+    fetch.wait()
 
     def spread(turn):
         if turn > 0:
@@ -288,36 +292,56 @@
     def dot(p, q):
         return lax.dot_general(p, q, contract, preferred_element_type=jnp.float32)
 
-    def compute(k, t):
-        r, j, swap = tile_of(k, t)
-        keep, _, _, _ = pair(r, j)
-        keep = jnp.logical_xor(keep, swap)
-        row = jnp.where(keep, r, slot_of(j))
-        col = jnp.where(keep, slot_of(j), r)
-        both = dot(hl[row], hl[col, :ROWS])
-        acc = both[:ROWS] + both[ROWS:] + dot(hl[row, :ROWS], hl[col, ROWS:])
-        index = GROUPS[k][0] + t
+    def put(index, acc):
         for xx in range(4):
             for yy in range(2):
                 start = 32 * xx + 16 * yy
                 pk[xx, index, yy] = acc[start : start + 16, :]
 
-    def d_copy(k):
+    def compute(k, p):
+        low, high = (0, 5) if p == 0 else (1, 4)
+        j = k if p == 0 else -k
+        slot = 0 if k == 0 else (UP[k] if p == 0 else DOWN[k])
+        n = high - low
+        tops = hl[low:high, :ROWS].reshape(n * ROWS, WIDTH)
+        rests = hl[low:high, ROWS:].reshape(n * ROWS, WIDTH)
+        both = dot(tops, hl[slot])
+        acc = both[:, :ROWS] + both[:, ROWS:] + dot(rests, hl[slot, :ROWS])
+        for r in range(low, high):
+            tile = acc[(r - low) * ROWS : (r - low + 1) * ROWS]
+            index = GROUPS[k][0] + (r if p == 0 else r + 4)
+            keep, _, _, _ = pair(r, j)
+
+            @pl.when(keep)
+            def _():
+                put(index, tile)
+
+            @pl.when(jnp.logical_not(keep))
+            def _():
+                put(index, tile.T)
+
+            if k == 0 and r == 2:
+                put(GROUPS[0][0] + 5, tile.T)
+
+    def some_tiles(k, p):
         t0, n = GROUPS[k]
-        tiles = pl.ds(t0, n)
-        return remote(pk.at[:, tiles], pr.at[:, tiles], d_send.at[k], d_recv.at[k], partner)
-
-    def x_copy(k, s):
-        t0, n = GROUPS[k]
+        if k in (0, 4):
+            return pl.ds(t0, n)
+        return pl.ds(t0, 5) if p == 0 else pl.ds(t0 + 5, 3)
+
+    def d_copy(k, p):
+        tiles = some_tiles(k, p)
+        return remote(pk.at[:, tiles], pr.at[:, tiles], d_send.at[k, p], d_recv.at[k, p], partner)
+
+    def x_copy(k, p, s):
+        tiles = some_tiles(k, p)
         return remote(
-            pk.at[rem(x + s, 4), pl.ds(t0, n)], xr.at[s - 1, pl.ds(t0, n)],
-            x_send.at[k], x_recv.at[k], at_x(s),
-        )
-
-    def over_cores(k):
-        t0, n = GROUPS[k]
-        tiles = pl.ds(t0, n)
-        landed(pr.at[:, tiles], d_recv.at[k])
+            pk.at[rem(x + s, 4), tiles], xr.at[s - 1, tiles], x_send.at[k, p], x_recv.at[k, p], at_x(s)
+        )
+
+    def over_cores(k, p):
+        tiles = some_tiles(k, p)
+        landed(pr.at[:, tiles], d_recv.at[k, p])
         pk[:, tiles] = pk[:, tiles] + pr[:, tiles]
 
     def target(k, t):
@@ -349,10 +373,10 @@
             g_send.at[t], g_recv.at[x, place], (*row, xx, hh),
         )
 
-    def over_planes(k):
-        t0, n = GROUPS[k]
-        tiles = pl.ds(t0, n)
-        landed(xr.at[:, tiles], x_recv.at[k])
+    def over_planes(k, p):
+        t0, _ = GROUPS[k]
+        tiles = some_tiles(k, p)
+        landed(xr.at[:, tiles], x_recv.at[k, p])
         fb[tiles] = (pk[x, tiles] + xr[0, tiles] + xr[1, tiles] + xr[2, tiles]) * (1.0 / NPARAMS)
 
         def send(t, carry):
@@ -370,7 +394,10 @@
 
             return carry
 
-        lax.fori_loop(0, n, send, 0)
+        if k == 0:
+            lax.fori_loop(0, 6, send, 0)
+        else:
+            lax.fori_loop(5 * p, 5 + 3 * p, send, 0)
 
     def go_home():
         def send(t, carry):
@@ -391,65 +418,68 @@
 
         lax.fori_loop(0, GROUPS[4][1], send, 0)
 
-    def some(k, start, stop):
-        lax.fori_loop(start, stop, lambda t, _: (compute(k, t), 0)[1], 0)
-
-    def convert_round(k):
-        if k == 0:
-            wait_mean()
-            lax.fori_loop(0, 5, lambda s, _: (convert(s), 0)[1], 0)
-        elif k < 4:
+    def convert_first():
+        wait_mean()
+        lax.fori_loop(0, 5, lambda s, _: (convert(s), 0)[1], 0)
+
+    @pl.when(other)
+    def _():
+        for i in range(2):
+            z_event(1, i)
+        convert_first()
+        for i in range(2, 4):
+            z_event(1, i)
+        compute(0, 0)
+        d_copy(0, 0).start()
+        for k in range(1, 4):
+            z_event(k + 1, 0)
+            convert(UP[k])
+            z_event(k + 1, 1)
+            compute(k, 0)
+            d_copy(k, 0).start()
+            z_event(k + 1, 2)
+            convert(DOWN[k])
+            compute(k, 1)
+            d_copy(k, 1).start()
+            z_event(k + 1, 3)
+        convert(UP[4])
+        compute(4, 0)
+        over_cores(4, 0)
+        go_home()
+
+    def plane_sums(k, p):
+        over_cores(k, p)
+        for s in range(1, 4):
+            x_copy(k, p, s).start()
+
+    @pl.when(first)
+    def _():
+        convert_first()
+        compute(0, 0)
+        for k in range(1, 4):
             convert(UP[k])
             convert(DOWN[k])
-        else:
-            convert(UP[4])
-
-    @pl.when(other)
-    def _():
-        for k in range(5):
-            n = GROUPS[k][1]
-            if k < 4:
-                z_event(k + 1, 0)
-            if k == 0:
-                z_event(1, 1)
-            convert_round(k)
-            if k == 0:
-                z_event(1, 2)
-            elif k < 4:
-                z_event(k + 1, 1)
-            some(k, 0, n // 2)
-            if k == 0:
-                z_event(1, 3)
-            elif k < 4:
-                z_event(k + 1, 2)
-            some(k, n // 2, n)
-            d_copy(k).start()
-            if 0 < k < 4:
-                z_event(k + 1, 3)
-
-    def plane_sums(k):
-        over_cores(k)
-        if k < 4:
-            for s in range(1, 4):
-                x_copy(k, s).start()
-        else:
-            go_home()
-
-    @pl.when(first)
-    def _():
-        for k in range(5):
-            if k == 4:
-                for i in range(NCH):
-                    z_event(4, i)
-            convert_round(k)
-            some(k, 0, GROUPS[k][1])
-            if k == 3:
-                plane_sums(0)
-        for k in range(1, 5):
-            plane_sums(k)
-            if k > 1:
-                over_planes(k - 2)
-        over_planes(3)
+            compute(k, 0)
+            compute(k, 1)
+        plane_sums(0, 0)
+        for i in range(NCH):
+            z_event(4, i)
+        convert(UP[4])
+        compute(4, 0)
+        d_copy(4, 0).start()
+        plane_sums(1, 0)
+        plane_sums(1, 1)
+        plane_sums(2, 0)
+        over_planes(0, 0)
+        plane_sums(2, 1)
+        over_planes(1, 0)
+        over_planes(1, 1)
+        plane_sums(3, 0)
+        plane_sums(3, 1)
+        over_planes(2, 0)
+        over_planes(2, 1)
+        over_planes(3, 0)
+        over_planes(3, 1)
 
     @pl.when(first)
     def _():
@@ -475,8 +505,9 @@
         remote(ys.at[pl.ds(0, 7)], ys.at[pl.ds(0, 7)], mt_send, mt_recv, at_z(1)).wait_send()
         for k in range(4):
             t0, n = GROUPS[k]
-            tiles = xr.at[:, pl.ds(t0, n)]
-            remote(tiles, tiles, x_send.at[k], x_recv.at[k], at_z(1)).wait_send()
+            for p in range(2 if k else 1):
+                tiles = xr.at[:, some_tiles(k, p)]
+                remote(tiles, tiles, x_send.at[k, p], x_recv.at[k, p], at_z(1)).wait_send()
 
             def gone(t, carry):
                 valid, mine, _, _ = target(k, t)
@@ -494,6 +525,14 @@
                 return carry
 
             lax.fori_loop(0, n, gone, 0)
+        d_copy(4, 0).wait_send()
+
+    @pl.when(other)
+    def _():
+        remote(ys, ys, mt_send, mt_recv, at_z(1)).wait_send()
+        for k in range(4):
+            for p in range(2 if k else 1):
+                d_copy(k, p).wait_send()
 
         def left(t, carry):
             valid, mine, _, _ = target(4, t)
@@ -511,12 +550,6 @@
             return carry
 
         lax.fori_loop(0, GROUPS[4][1], left, 0)
-
-    @pl.when(other)
-    def _():
-        remote(ys, ys, mt_send, mt_recv, at_z(1)).wait_send()
-        for k in range(5):
-            d_copy(k).wait_send()
 
     def arrived(d, carry):
         step = div(d, 2)
@@ -539,7 +572,7 @@
     for place in range(4):
         d = 16 * (place // 2) + 8 + (place % 2) - c
         for xx in range(4):
-            @pl.when(jnp.logical_not(first & (d == 8) & (z < 4) & (x == xx)))
+            @pl.when(jnp.logical_not(other & (d == 9) & (h == 1) & (z < 4) & (x == xx)))
             def _():
                 landed(home.at[xx, place], g_recv.at[xx, place])
         total = home[0, place] + home[1, place] + home[2, place] + home[3, place]
@@ -552,9 +585,10 @@
     return pl.pallas_call(
         kernel,
         out_shape=jax.ShapeDtypeStruct((1, HALF + 1, 16, ROWS), f32),
-        in_specs=[pl.BlockSpec(memory_space=pltpu.VMEM)],
+        in_specs=[pl.BlockSpec(memory_space=pl.ANY)],
         out_specs=pl.BlockSpec(memory_space=pltpu.VMEM),
         scratch_shapes=[
+            pltpu.VMEM((ROWS, WIDTH), f32),
             pltpu.VMEM((NSLOT, ROWS, WIDTH), f32),
             pltpu.VMEM((NSLOT, 2 * ROWS, WIDTH), bf16),
             pltpu.VMEM((8, 8, LANES), f32),
@@ -577,10 +611,11 @@
             dma(()),
             dma(()),
             pltpu.SemaphoreType.REGULAR((4,)),
-            dma((5,)),
-            dma((5,)),
-            dma((4,)),
-            dma((4,)),
+            dma(()),
+            dma((5, 2)),
+            dma((5, 2)),
+            dma((4, 2)),
+            dma((4, 2)),
             dma((NTILE,)),
             dma((HALF + 1,)),
             dma((5,)),

time: 72.8 us -> 69.2 us (0.951)
  Pallas kernels: 70.9 us -> 67.3 us
    pallas_call x1, Pallas kernels: 70.9 us -> 67.3 us  [on_device(): pl.pallas_call(kernel, out_shape=jax.ShapeDtypeStruct((1, HALF + 1, 16, R...]
where the time goes in v4:
time: 69.2 us; the launch traced here: 69 us
  Pallas kernels  67.3 us (97%)
  local copies, waits for them, and re-layouts  1.68 us (2%)
    pallas_call x1, Pallas kernels, on_device(): pl.pallas_call(kernel, out_shape=jax.ShapeDtypeStruct((1, HALF + 1, 16, R...  67.3 us
    unnamed x1, local copies, waits for them, and re-layouts  1.68 us

profile of v4, /device:TPU:1, one launch (start us, length us, event | category | flops | bytes accessed | tf_op | source)
XLA Modules:
  0.0 69.0 jit_solution(5062943115273324744)
XLA Ops:
  0.0 67.3 %shard_map.17 = f32[1,33,16,128]{3,2,1,0:T(8,128)} custom-call(f32[128,768]{1,0:T(8,128)} %x_hbm.1), custom_call_target="tpu_custom_call" | custom-call | tf_op jit(solution)/shard_map/pallas_call | solution.py:585
  67.3 1.7 %copy.3 = f32[1,33,16,128]{3,2,1,0:T(8,128)} copy(f32[1,33,16,128]{3,2,1,0:T(8,128)} %shard_map.17) | data formatting | bytes 540672

commit v5 on v4

--- a/solution.py
+++ b/solution.py
@@ -584,7 +584,7 @@
     dma = pltpu.SemaphoreType.DMA
     return pl.pallas_call(
         kernel,
-        out_shape=jax.ShapeDtypeStruct((1, HALF + 1, 16, ROWS), f32),
+        out_shape=pltpu.VMEM((1, HALF + 1, 16, ROWS), f32),
         in_specs=[pl.BlockSpec(memory_space=pl.ANY)],
         out_specs=pl.BlockSpec(memory_space=pltpu.VMEM),
         scratch_shapes=[

time: 69.2 us -> 67.4 us (0.974)
  local copies, waits for them, and re-layouts: 1.68 us -> 0.71 us
  Pallas kernels: 67.3 us -> 66.6 us
    unnamed x1, local copies, waits for them, and re-layouts: 1.68 us -> 0.71 us
    pallas_call x1, Pallas kernels: 67.3 us -> 66.6 us  [on_device(): pl.pallas_call(kernel, out_shape=pltpu.VMEM((1, HALF + 1, 16, ROWS), f32)...]
where the time goes in v5:
time: 67.4 us; the launch traced here: 67.3 us
  Pallas kernels  66.6 us (99%)
  local copies, waits for them, and re-layouts  0.71 us (1%)
    pallas_call x1, Pallas kernels, on_device(): pl.pallas_call(kernel, out_shape=pltpu.VMEM((1, HALF + 1, 16, ROWS), f32)...  66.6 us

profile of v5, /device:TPU:1, one launch (start us, length us, event | category | flops | bytes accessed | tf_op | source)
XLA Modules:
  0.0 67.3 jit_solution(2230339102528892038)
XLA Ops:
  0.0 66.6 %shard_map.17 = f32[1,33,16,128]{3,2,1,0:T(8,128)S(1)} custom-call(f32[128,768]{1,0:T(8,128)} %x_hbm.1), custom_call_target="tpu_custom_call" | custom-call | tf_op jit(solution)/shard_map/pallas_call | solution.py:585
  66.6 0.7 %copy.3 = f32[1,33,16,128]{3,2,1,0:T(8,128)} copy(f32[1,33,16,128]{3,2,1,0:T(8,128)S(1)} %shard_map.17) | data formatting | bytes 540672
